TPU v7x, 32 devices: a whole 2x2x4 slice. The times are simulated.
32 devices in a mesh: pb: 8 (over y, x, core), ga: 4 (over z).
Axes of the slice: x: 2, y: 2, z: 4, core: 2. Of those that a mesh axis runs over, the one named last changes fastest.
Arguments:
- query_points: float32 [3, 32768], P(None, 'pb'), may hold values from 0 to 1
- cotangent: bfloat16 [64, 32768], P(None, 'pb'), may hold values from -6 to 6
- slab_ids: int32 [8, 32768], P(None, 'pb'), may hold values from -1 to 3
- rel_cells: int32 [8, 32768], P(None, 'pb'), may hold values from 0 to 511
- offsets: int32 [4, 256], P('ga', 'pb'), may hold values from 0 to 15872
- latent: bfloat16 [4, 64, 16384], P('ga', None, 'pb'), may hold values from -6 to 6
- w_in: float32 [80, 6], replicated, may hold values from -2.5 to 2.5
- b_in: float32 [80], replicated, may hold values from -3 to 3
- w_out: bfloat16 [64, 80], replicated, may hold values from -0.625 to 0.625
- b_out: float32 [64], replicated, may hold values from -3 to 3
Outputs:
- grid_grad: float32 [4, 64, 16384], P('ga', None, 'pb')
- w_in_grad: float32 [80, 6], replicated
- b_in_grad: float32 [80], replicated
- w_out_grad: float32 [64, 80], replicated
- b_out_grad: float32 [64], replicated
Inputs may be any that keep to these rules, and one draw needn't show every extreme that they name: `slab_ids`: -1 marks a padding slot; otherwise the slab that holds the neighbour cell.
All inputs are finite; a program needn't handle non-finite values.
Results may differ from a plain program's by a relative error of at most 0.0085.
Values may be sent and summed in bfloat16 or wider, within the bound.
A program may use at most 64 MiB of HBM per device.

v0:
```python
import math

import jax
import jax.numpy as jnp
from jax import lax
from jax.sharding import PartitionSpec as P

KN = 8
TILE = 128
WIN = 512
GX = 64
ZS = 4


def gelu_exact(values):
    return jax.nn.gelu(values, approximate=False)


def shards(query_points, cotangent, slab_ids, rel_cells, offsets, latent, w_in, b_in, w_out, b_out):
    channels = latent.shape[1]
    slab_feats = lax.all_gather(latent, "pb", axis=2, tiled=True)[0]
    cells_slab = slab_feats.shape[1]
    slab_here = lax.axis_index("ga")
    queries_dev = query_points.shape[1]
    tiles_dev = queries_dev // TILE
    per_block = math.gcd(tiles_dev, 4)
    blocks = tiles_dev // per_block
    entries = KN * TILE

    def reshape_tiles(values):
        leading = values.shape[0]
        return values.reshape(leading, blocks, per_block, TILE).transpose(1, 2, 0, 3)

    def tile_work(anchor, points, cot_cols, slabs, rels):
        window = lax.dynamic_slice_in_dim(slab_feats, anchor, WIN, 1)
        rel_flat = rels.reshape(-1)
        live_flat = slabs.reshape(-1) == slab_here
        onehot = (
            (lax.broadcasted_iota(jnp.int32, (WIN, entries), 0) == rel_flat[None, :])
            & live_flat[None, :]
        ).astype(jnp.bfloat16)
        feats = jnp.dot(window, onehot, preferred_element_type=jnp.float32)
        cell = anchor + rel_flat
        along_x = cell // (GX * ZS)
        along_y = cell // ZS % GX
        along_z = cell % ZS + slab_here * ZS
        centres = jnp.stack(
            [
                (along_x.astype(jnp.float32) + 0.5) / GX,
                (along_y.astype(jnp.float32) + 0.5) / GX,
                (along_z.astype(jnp.float32) + 0.5) / GX,
            ],
            0,
        )
        features_in = jnp.concatenate([jnp.tile(points, (1, KN)), centres], 0)
        mask_flat = live_flat.astype(jnp.float32)
        cot_flat = jnp.tile(cot_cols.astype(jnp.float32), (1, KN))
        preact = (
            jnp.dot(
                w_in,
                features_in,
                precision=lax.Precision.HIGHEST,
                preferred_element_type=jnp.float32,
            )
            + b_in[:, None]
        )
        hidden = gelu_exact(preact).astype(jnp.bfloat16)
        kernel = jnp.dot(w_out, hidden, preferred_element_type=jnp.float32) + b_out[:, None]
        grad_cell = (kernel * cot_flat * mask_flat).astype(jnp.bfloat16)
        grad_kernel = (feats * cot_flat * mask_flat).astype(jnp.bfloat16)
        window_grad = lax.dot_general(
            grad_cell, onehot, (((1,), (1,)), ((), ())), preferred_element_type=jnp.float32
        )
        grad_w_out = lax.dot_general(
            grad_kernel, hidden, (((1,), (1,)), ((), ())), preferred_element_type=jnp.float32
        )
        grad_b_out = jnp.sum(grad_kernel.astype(jnp.float32), 1)
        grad_hidden = lax.dot_general(
            w_out, grad_kernel, (((0,), (0,)), ((), ())), preferred_element_type=jnp.float32
        )
        grad_pre = jax.vjp(gelu_exact, preact)[1](grad_hidden)[0]
        grad_w_in = lax.dot_general(
            grad_pre,
            features_in,
            (((1,), (1,)), ((), ())),
            precision=lax.Precision.HIGHEST,
            preferred_element_type=jnp.float32,
        )
        grad_b_in = jnp.sum(grad_pre, 1)
        return (window_grad, grad_w_in, grad_b_in, grad_w_out, grad_b_out)

    def advance(running, inputs_block):
        partial_grad, totals = running
        anchors, points, cot_cols, slabs, rels = inputs_block
        results = jax.vmap(tile_work)(anchors, points, cot_cols, slabs, rels)
        for number in range(per_block):
            current = lax.dynamic_slice_in_dim(partial_grad, anchors[number], WIN, 1)
            partial_grad = lax.dynamic_update_slice_in_dim(
                partial_grad, current + results[0][number], anchors[number], 1
            )
        totals = tuple((old + jnp.sum(new, 0) for old, new in zip(totals, results[1:])))
        return ((partial_grad, totals), None)

    start_totals = (
        jnp.zeros((w_in.shape[0], 6), jnp.float32),
        jnp.zeros((w_in.shape[0],), jnp.float32),
        jnp.zeros((channels, w_in.shape[0]), jnp.float32),
        jnp.zeros((channels,), jnp.float32),
    )
    start_grid = jnp.zeros((channels, cells_slab), jnp.float32)
    inputs_all = (
        offsets[0].reshape(blocks, per_block),
        reshape_tiles(query_points),
        reshape_tiles(cotangent),
        reshape_tiles(slab_ids),
        reshape_tiles(rel_cells),
    )
    (partial_grad, totals), _ = lax.scan(advance, (start_grid, start_totals), inputs_all)
    owned = lax.psum_scatter(partial_grad, "pb", scatter_dimension=1, tiled=True)
    sums = lax.psum((totals[0], totals[1], totals[2], totals[3]), ("pb", "ga"))
    scale = float(queries_dev * lax.axis_size("pb")) ** (-0.5)
    return (owned[None], sums[0] * scale, sums[1] * scale, sums[2] * scale, sums[3] * scale)


def solution(mesh):
    return jax.shard_map(
        shards,
        mesh=mesh,
        in_specs=(
            P(None, "pb"),
            P(None, "pb"),
            P(None, "pb"),
            P(None, "pb"),
            P("ga", "pb"),
            P("ga", None, "pb"),
            P(),
            P(),
            P(),
            P(),
        ),
        out_specs=(P("ga", None, "pb"), P(), P(), P(), P()),
        check_vma=False,
    )
```

profile of v0, /device:TPU:0, one launch (start us, length us, event | category | flops | bytes accessed | tf_op | source)
XLA Modules:
  0.0 460.4 jit_solution(14225851162701294720)
XLA Ops:
  12.2 28.2 %all-gather.2.cloned.1.call-done = bf16[1,64,16384]{2,1,0:T(8,128)(2,1)} async-done(((bf16[1,64,2048]{2,1,0:T(8,128)(2,1)}), bf16[1,64,16384]{2,1,0:T(8,128)(2,1)}) %all-gather.2.cloned.1.call-update) | async-done | bytes 2097168 | tf_op jit(solution)/shard_map/all_gather | solution.py:21
  42.7 358.9 %while.26 = (s32[]{:T(128)}, f32[64,16384]{1,0:T(8,128)}, f32[80,6]{0,1:T(8,128)S(1)}, f32[80]{0:T(128)S(1)}, f32[64,80]{1,0:T(8,128)S(1)}, /*index=5*/f32[64]{0...) while((s32[]{:T(128)}, f32[64,16384]{1,0:T(8,128)}, ...), condition=%wide.region_3.4_spmd.clone, body=%wide.region_0.3_spmd.clone.sunk | while | flops 747289728 | bytes 25849020 | solution.py:118
  52.8 8.9 %while.27 = (s32[]{:T(128)}, bf16[64,16384]{1,0:T(8,128)(2,1)}, s32[4,2]{0,1:T(2,128)S(1)}, bf16[4,64,512]{2,1,0:T(8,128)(2,1)S(1)}, s32[]{:T(128)}) while((s32[]{:T(128)}, bf16[64,16384]{1,0:T(8,128)(2,1)}, s32[4,2]{0,1:T(2,128)S(1)}, bf16[4,64,512]{2,1,0:T(8,128)(2,1)S(1)}, s32[]{:T(128)}) %tuple.81), condition=%wide.while_cond, body=%wide.while_body.sunk | while | flops 2 | bytes 131177 | solution.py:35
  64.3 5.4 %fusion.121 = (bf16[4,80,1024]{2,1,0:T(8,128)(2,1)S(1)}, f32[4,80,1024]{2,1,0:T(8,128)}, f32[4,1024,80]{1,2,0:T(8,128)}) fusion(f32[80]{0:T(128)S(1)} %get-tuple-element.726, f32[80,6]{0,1:T(8,128)S(1)} %get-tuple-element.725, f32[4,6,1024]{2,0,1:T(4,128)S(1)} %pad_maximum_fusion.2), kind=kOutput, calls=%fused_computation.27.clone.1 | convolution fusion | flops 45219840 | bytes 3377344 | tf_op jit(solution)/shard_map/while/body/eval_jaxpr/vmap()/dot_general | solution.py:59
  69.6 2.3 fusion.122
  71.9 2.6 fusion.128
  97.5 8.9 %while.27 = (s32[]{:T(128)}, bf16[64,16384]{1,0:T(8,128)(2,1)}, s32[4,2]{0,1:T(2,128)S(1)}, bf16[4,64,512]{2,1,0:T(8,128)(2,1)S(1)}, s32[]{:T(128)}) while((s32[]{:T(128)}, bf16[64,16384]{1,0:T(8,128)(2,1)}, s32[4,2]{0,1:T(2,128)S(1)}, bf16[4,64,512]{2,1,0:T(8,128)(2,1)S(1)}, s32[]{:T(128)}) %tuple.81), condition=%wide.while_cond, body=%wide.while_body.sunk | while | flops 2 | bytes 131177 | solution.py:35
  109.0 5.4 %fusion.121 = (bf16[4,80,1024]{2,1,0:T(8,128)(2,1)S(1)}, f32[4,80,1024]{2,1,0:T(8,128)}, f32[4,1024,80]{1,2,0:T(8,128)}) fusion(f32[80]{0:T(128)S(1)} %get-tuple-element.726, f32[80,6]{0,1:T(8,128)S(1)} %get-tuple-element.725, f32[4,6,1024]{2,0,1:T(4,128)S(1)} %pad_maximum_fusion.2), kind=kOutput, calls=%fused_computation.27.clone.1 | convolution fusion | flops 45219840 | bytes 3377344 | tf_op jit(solution)/shard_map/while/body/eval_jaxpr/vmap()/dot_general | solution.py:59
  116.6 2.6 fusion.128
  142.4 8.9 %while.27 = (s32[]{:T(128)}, bf16[64,16384]{1,0:T(8,128)(2,1)}, s32[4,2]{0,1:T(2,128)S(1)}, bf16[4,64,512]{2,1,0:T(8,128)(2,1)S(1)}, s32[]{:T(128)}) while((s32[]{:T(128)}, bf16[64,16384]{1,0:T(8,128)(2,1)}, s32[4,2]{0,1:T(2,128)S(1)}, bf16[4,64,512]{2,1,0:T(8,128)(2,1)S(1)}, s32[]{:T(128)}) %tuple.81), condition=%wide.while_cond, body=%wide.while_body.sunk | while | flops 2 | bytes 131177 | solution.py:35
  153.9 5.4 %fusion.121 = (bf16[4,80,1024]{2,1,0:T(8,128)(2,1)S(1)}, f32[4,80,1024]{2,1,0:T(8,128)}, f32[4,1024,80]{1,2,0:T(8,128)}) fusion(f32[80]{0:T(128)S(1)} %get-tuple-element.726, f32[80,6]{0,1:T(8,128)S(1)} %get-tuple-element.725, f32[4,6,1024]{2,0,1:T(4,128)S(1)} %pad_maximum_fusion.2), kind=kOutput, calls=%fused_computation.27.clone.1 | convolution fusion | flops 45219840 | bytes 3377344 | tf_op jit(solution)/shard_map/while/body/eval_jaxpr/vmap()/dot_general | solution.py:59
  161.5 2.6 fusion.128
  187.3 8.9 %while.27 = (s32[]{:T(128)}, bf16[64,16384]{1,0:T(8,128)(2,1)}, s32[4,2]{0,1:T(2,128)S(1)}, bf16[4,64,512]{2,1,0:T(8,128)(2,1)S(1)}, s32[]{:T(128)}) while((s32[]{:T(128)}, bf16[64,16384]{1,0:T(8,128)(2,1)}, s32[4,2]{0,1:T(2,128)S(1)}, bf16[4,64,512]{2,1,0:T(8,128)(2,1)S(1)}, s32[]{:T(128)}) %tuple.81), condition=%wide.while_cond, body=%wide.while_body.sunk | while | flops 2 | bytes 131177 | solution.py:35
  198.7 5.4 %fusion.121 = (bf16[4,80,1024]{2,1,0:T(8,128)(2,1)S(1)}, f32[4,80,1024]{2,1,0:T(8,128)}, f32[4,1024,80]{1,2,0:T(8,128)}) fusion(f32[80]{0:T(128)S(1)} %get-tuple-element.726, f32[80,6]{0,1:T(8,128)S(1)} %get-tuple-element.725, f32[4,6,1024]{2,0,1:T(4,128)S(1)} %pad_maximum_fusion.2), kind=kOutput, calls=%fused_computation.27.clone.1 | convolution fusion | flops 45219840 | bytes 3377344 | tf_op jit(solution)/shard_map/while/body/eval_jaxpr/vmap()/dot_general | solution.py:59
  204.1 2.3 fusion.122
  206.4 2.6 fusion.128
  232.2 8.9 %while.27 = (s32[]{:T(128)}, bf16[64,16384]{1,0:T(8,128)(2,1)}, s32[4,2]{0,1:T(2,128)S(1)}, bf16[4,64,512]{2,1,0:T(8,128)(2,1)S(1)}, s32[]{:T(128)}) while((s32[]{:T(128)}, bf16[64,16384]{1,0:T(8,128)(2,1)}, s32[4,2]{0,1:T(2,128)S(1)}, bf16[4,64,512]{2,1,0:T(8,128)(2,1)S(1)}, s32[]{:T(128)}) %tuple.81), condition=%wide.while_cond, body=%wide.while_body.sunk | while | flops 2 | bytes 131177 | solution.py:35
  243.6 5.4 %fusion.121 = (bf16[4,80,1024]{2,1,0:T(8,128)(2,1)S(1)}, f32[4,80,1024]{2,1,0:T(8,128)}, f32[4,1024,80]{1,2,0:T(8,128)}) fusion(f32[80]{0:T(128)S(1)} %get-tuple-element.726, f32[80,6]{0,1:T(8,128)S(1)} %get-tuple-element.725, f32[4,6,1024]{2,0,1:T(4,128)S(1)} %pad_maximum_fusion.2), kind=kOutput, calls=%fused_computation.27.clone.1 | convolution fusion | flops 45219840 | bytes 3377344 | tf_op jit(solution)/shard_map/while/body/eval_jaxpr/vmap()/dot_general | solution.py:59
  249.0 2.3 fusion.122
  251.3 2.6 fusion.128
  277.1 8.9 %while.27 = (s32[]{:T(128)}, bf16[64,16384]{1,0:T(8,128)(2,1)}, s32[4,2]{0,1:T(2,128)S(1)}, bf16[4,64,512]{2,1,0:T(8,128)(2,1)S(1)}, s32[]{:T(128)}) while((s32[]{:T(128)}, bf16[64,16384]{1,0:T(8,128)(2,1)}, s32[4,2]{0,1:T(2,128)S(1)}, bf16[4,64,512]{2,1,0:T(8,128)(2,1)S(1)}, s32[]{:T(128)}) %tuple.81), condition=%wide.while_cond, body=%wide.while_body.sunk | while | flops 2 | bytes 131177 | solution.py:35
  288.5 5.4 %fusion.121 = (bf16[4,80,1024]{2,1,0:T(8,128)(2,1)S(1)}, f32[4,80,1024]{2,1,0:T(8,128)}, f32[4,1024,80]{1,2,0:T(8,128)}) fusion(f32[80]{0:T(128)S(1)} %get-tuple-element.726, f32[80,6]{0,1:T(8,128)S(1)} %get-tuple-element.725, f32[4,6,1024]{2,0,1:T(4,128)S(1)} %pad_maximum_fusion.2), kind=kOutput, calls=%fused_computation.27.clone.1 | convolution fusion | flops 45219840 | bytes 3377344 | tf_op jit(solution)/shard_map/while/body/eval_jaxpr/vmap()/dot_general | solution.py:59
  296.2 2.6 fusion.128
  321.9 8.9 %while.27 = (s32[]{:T(128)}, bf16[64,16384]{1,0:T(8,128)(2,1)}, s32[4,2]{0,1:T(2,128)S(1)}, bf16[4,64,512]{2,1,0:T(8,128)(2,1)S(1)}, s32[]{:T(128)}) while((s32[]{:T(128)}, bf16[64,16384]{1,0:T(8,128)(2,1)}, s32[4,2]{0,1:T(2,128)S(1)}, bf16[4,64,512]{2,1,0:T(8,128)(2,1)S(1)}, s32[]{:T(128)}) %tuple.81), condition=%wide.while_cond, body=%wide.while_body.sunk | while | flops 2 | bytes 131177 | solution.py:35
  333.4 5.4 %fusion.121 = (bf16[4,80,1024]{2,1,0:T(8,128)(2,1)S(1)}, f32[4,80,1024]{2,1,0:T(8,128)}, f32[4,1024,80]{1,2,0:T(8,128)}) fusion(f32[80]{0:T(128)S(1)} %get-tuple-element.726, f32[80,6]{0,1:T(8,128)S(1)} %get-tuple-element.725, f32[4,6,1024]{2,0,1:T(4,128)S(1)} %pad_maximum_fusion.2), kind=kOutput, calls=%fused_computation.27.clone.1 | convolution fusion | flops 45219840 | bytes 3377344 | tf_op jit(solution)/shard_map/while/body/eval_jaxpr/vmap()/dot_general | solution.py:59
  341.0 2.6 fusion.128
  366.8 8.9 %while.27 = (s32[]{:T(128)}, bf16[64,16384]{1,0:T(8,128)(2,1)}, s32[4,2]{0,1:T(2,128)S(1)}, bf16[4,64,512]{2,1,0:T(8,128)(2,1)S(1)}, s32[]{:T(128)}) while((s32[]{:T(128)}, bf16[64,16384]{1,0:T(8,128)(2,1)}, s32[4,2]{0,1:T(2,128)S(1)}, bf16[4,64,512]{2,1,0:T(8,128)(2,1)S(1)}, s32[]{:T(128)}) %tuple.81), condition=%wide.while_cond, body=%wide.while_body.sunk | while | flops 2 | bytes 131177 | solution.py:35
  378.2 5.4 %fusion.121 = (bf16[4,80,1024]{2,1,0:T(8,128)(2,1)S(1)}, f32[4,80,1024]{2,1,0:T(8,128)}, f32[4,1024,80]{1,2,0:T(8,128)}) fusion(f32[80]{0:T(128)S(1)} %get-tuple-element.726, f32[80,6]{0,1:T(8,128)S(1)} %get-tuple-element.725, f32[4,6,1024]{2,0,1:T(4,128)S(1)} %pad_maximum_fusion.2), kind=kOutput, calls=%fused_computation.27.clone.1 | convolution fusion | flops 45219840 | bytes 3377344 | tf_op jit(solution)/shard_map/while/body/eval_jaxpr/vmap()/dot_general | solution.py:59
  383.6 2.3 fusion.122
  385.9 2.6 fusion.128
  401.6 40.2 %all-reduce.1 = (f32[80,6]{0,1:T(8,128)S(1)}, f32[80]{0:T(128)S(1)}, f32[64,80]{1,0:T(8,128)S(1)}, f32[64]{0:T(128)S(1)}) all-reduce(f32[80,6]{0,1:T(8,128)S(1)} %get-tuple-element.285, f32[80]{0:T(128)S(1)} %get-tuple-element.286, f32[64,80]{1,0:T(8,128)S(1)} %get-tuple-element.287, ...), channel_id=1, replica_groups=mesh['pb'=8,'ga'=4] {'pb','ga'}, use_global_device_ids=true, to_apply=%region_5.6 | all-reduce | flops 5744 | bytes 45952 | tf_op jit(solution)/shard_map/psum | solution.py:120
  444.1 9.5 %reduce-scatter.2.cloned.1.call-done = f32[64,2048]{1,0:T(8,128)} async-done(((f32[64,16384]{1,0:T(8,128)}), f32[64,2048]{1,0:T(8,128)}) %reduce-scatter.2.cloned.1.call-update) | async-done | bytes 524304 | tf_op jit(solution)/shard_map/reduce_scatter | solution.py:119
  (414 shorter events, 233.0 us)
Async XLA Ops:
  7.2 33.2 %all-gather.2.cloned.1.call-start = ((), (), s32[]{:S(2)}) async-start(), calls=%async_computation.1 | async-start | bytes 2359296 | tf_op jit(solution)/shard_map/all_gather | solution.py:21
  7.9 445.7 %reduce-scatter.2.cloned.1.call-start = ((), (), s32[]{:S(2)}) async-start(), calls=%async_computation.2 | async-start | bytes 4718592 | tf_op jit(solution)/shard_map/reduce_scatter | solution.py:119
  40.4 2.3 copy-start.2
  40.4 2.3 copy-start.3
  40.4 2.3 copy-start.4
  40.4 2.3 copy-start.5
  42.7 19.1 %copy-start = (bf16[8,4,64,128]{3,1,0,2:T(4,128)(2,1)}, bf16[8,4,64,128]{3,1,0,2:T(4,128)(2,1)S(1)}, u32[]{:S(2)}) copy-start(bf16[8,4,64,128]{3,1,0,2:T(4,128)(2,1)S(1)} %get-tuple-element.729) | copy-start | bytes 1572868 | tf_op jit(solution)/shard_map/while
  76.0 11.4 %copy-start.1 = (bf16[8,4,64,128]{3,1,0,2:T(4,128)(2,1)S(1)}, bf16[8,4,64,128]{3,1,0,2:T(4,128)(2,1)}, u32[]{:S(2)}) copy-start(bf16[8,4,64,128]{3,1,0,2:T(4,128)(2,1)} %copy-done) | copy-start | bytes 1572868 | tf_op jit(solution)/shard_map/while
  87.4 19.0 %copy-start = (bf16[8,4,64,128]{3,1,0,2:T(4,128)(2,1)}, bf16[8,4,64,128]{3,1,0,2:T(4,128)(2,1)S(1)}, u32[]{:S(2)}) copy-start(bf16[8,4,64,128]{3,1,0,2:T(4,128)(2,1)S(1)} %get-tuple-element.729) | copy-start | bytes 1572868 | tf_op jit(solution)/shard_map/while
  120.7 11.6 %copy-start.1 = (bf16[8,4,64,128]{3,1,0,2:T(4,128)(2,1)S(1)}, bf16[8,4,64,128]{3,1,0,2:T(4,128)(2,1)}, u32[]{:S(2)}) copy-start(bf16[8,4,64,128]{3,1,0,2:T(4,128)(2,1)} %copy-done) | copy-start | bytes 1572868 | tf_op jit(solution)/shard_map/while
  132.3 19.0 %copy-start = (bf16[8,4,64,128]{3,1,0,2:T(4,128)(2,1)}, bf16[8,4,64,128]{3,1,0,2:T(4,128)(2,1)S(1)}, u32[]{:S(2)}) copy-start(bf16[8,4,64,128]{3,1,0,2:T(4,128)(2,1)S(1)} %get-tuple-element.729) | copy-start | bytes 1572868 | tf_op jit(solution)/shard_map/while
  165.6 11.6 %copy-start.1 = (bf16[8,4,64,128]{3,1,0,2:T(4,128)(2,1)S(1)}, bf16[8,4,64,128]{3,1,0,2:T(4,128)(2,1)}, u32[]{:S(2)}) copy-start(bf16[8,4,64,128]{3,1,0,2:T(4,128)(2,1)} %copy-done) | copy-start | bytes 1572868 | tf_op jit(solution)/shard_map/while
  177.2 19.0 %copy-start = (bf16[8,4,64,128]{3,1,0,2:T(4,128)(2,1)}, bf16[8,4,64,128]{3,1,0,2:T(4,128)(2,1)S(1)}, u32[]{:S(2)}) copy-start(bf16[8,4,64,128]{3,1,0,2:T(4,128)(2,1)S(1)} %get-tuple-element.729) | copy-start | bytes 1572868 | tf_op jit(solution)/shard_map/while
  210.5 11.6 %copy-start.1 = (bf16[8,4,64,128]{3,1,0,2:T(4,128)(2,1)S(1)}, bf16[8,4,64,128]{3,1,0,2:T(4,128)(2,1)}, u32[]{:S(2)}) copy-start(bf16[8,4,64,128]{3,1,0,2:T(4,128)(2,1)} %copy-done) | copy-start | bytes 1572868 | tf_op jit(solution)/shard_map/while
  222.1 19.0 %copy-start = (bf16[8,4,64,128]{3,1,0,2:T(4,128)(2,1)}, bf16[8,4,64,128]{3,1,0,2:T(4,128)(2,1)S(1)}, u32[]{:S(2)}) copy-start(bf16[8,4,64,128]{3,1,0,2:T(4,128)(2,1)S(1)} %get-tuple-element.729) | copy-start | bytes 1572868 | tf_op jit(solution)/shard_map/while
  255.4 11.6 %copy-start.1 = (bf16[8,4,64,128]{3,1,0,2:T(4,128)(2,1)S(1)}, bf16[8,4,64,128]{3,1,0,2:T(4,128)(2,1)}, u32[]{:S(2)}) copy-start(bf16[8,4,64,128]{3,1,0,2:T(4,128)(2,1)} %copy-done) | copy-start | bytes 1572868 | tf_op jit(solution)/shard_map/while
  267.0 19.0 %copy-start = (bf16[8,4,64,128]{3,1,0,2:T(4,128)(2,1)}, bf16[8,4,64,128]{3,1,0,2:T(4,128)(2,1)S(1)}, u32[]{:S(2)}) copy-start(bf16[8,4,64,128]{3,1,0,2:T(4,128)(2,1)S(1)} %get-tuple-element.729) | copy-start | bytes 1572868 | tf_op jit(solution)/shard_map/while
  300.3 11.6 %copy-start.1 = (bf16[8,4,64,128]{3,1,0,2:T(4,128)(2,1)S(1)}, bf16[8,4,64,128]{3,1,0,2:T(4,128)(2,1)}, u32[]{:S(2)}) copy-start(bf16[8,4,64,128]{3,1,0,2:T(4,128)(2,1)} %copy-done) | copy-start | bytes 1572868 | tf_op jit(solution)/shard_map/while
  311.8 19.0 %copy-start = (bf16[8,4,64,128]{3,1,0,2:T(4,128)(2,1)}, bf16[8,4,64,128]{3,1,0,2:T(4,128)(2,1)S(1)}, u32[]{:S(2)}) copy-start(bf16[8,4,64,128]{3,1,0,2:T(4,128)(2,1)S(1)} %get-tuple-element.729) | copy-start | bytes 1572868 | tf_op jit(solution)/shard_map/while
  345.1 11.6 %copy-start.1 = (bf16[8,4,64,128]{3,1,0,2:T(4,128)(2,1)S(1)}, bf16[8,4,64,128]{3,1,0,2:T(4,128)(2,1)}, u32[]{:S(2)}) copy-start(bf16[8,4,64,128]{3,1,0,2:T(4,128)(2,1)} %copy-done) | copy-start | bytes 1572868 | tf_op jit(solution)/shard_map/while
  356.7 19.0 %copy-start = (bf16[8,4,64,128]{3,1,0,2:T(4,128)(2,1)}, bf16[8,4,64,128]{3,1,0,2:T(4,128)(2,1)S(1)}, u32[]{:S(2)}) copy-start(bf16[8,4,64,128]{3,1,0,2:T(4,128)(2,1)S(1)} %get-tuple-element.729) | copy-start | bytes 1572868 | tf_op jit(solution)/shard_map/while
  390.0 11.6 %copy-start.1 = (bf16[8,4,64,128]{3,1,0,2:T(4,128)(2,1)S(1)}, bf16[8,4,64,128]{3,1,0,2:T(4,128)(2,1)}, u32[]{:S(2)}) copy-start(bf16[8,4,64,128]{3,1,0,2:T(4,128)(2,1)} %copy-done) | copy-start | bytes 1572868 | tf_op jit(solution)/shard_map/while
Sparse Core Ops, SparseCore 0:
  9.9 30.4 all-gather.1
  401.7 51.7 reduce-scatter.1
where the time goes:
time: 465 us; the launch traced here: 460 us
  local copies, waits for them, and re-layouts  149 us (32%)
  matrix products  112 us (24%)
  loops' own time  62.8 us (14%)
  other arithmetic  44.2 us (10%)
  blocking collectives  40.2 us (9%)
  waiting for transfers between devices  38.4 us (8%)
  between operations  14.1 us (3%)
    gather x96, local copies, waits for them, and re-layouts  70.8 us
    another operation x1, loops' own time, shards(): lax.scan(advance, (start_grid, start_totals), inputs_all)  62.1 us
    dynamic_update_slice x32, local copies, waits for them, and re-layouts, advance(): lax.dynamic_update_slice_in_dim(partial_grad, current + results[0][number...  59.2 us
    dot_general x8, matrix products, tile_work(): jnp.dot(w_in, features_in, precision=lax.Precision.HIGHEST, preferred_ele...  43 us
    psum x1, blocking collectives, shards(): sums = lax.psum((totals[0], totals[1], totals[2], totals[3]), ('pb', 'ga'))  40.2 us
    add x32, other arithmetic, advance(): current + results[0][number]  32.9 us
    all_gather x1, waiting for transfers between devices, shards(): slab_feats = lax.all_gather(latent, 'pb', axis=2, tiled=True)[0]  28.2 us
    dot_general x8, matrix products, tile_work(): lax.dot_general(w_out, grad_kernel, (((0,), (0,)), ((), ())), preferred_e...  20.4 us
  transfers between devices with their start and end apart: 2, of which 2 were waited for; matrix products, arithmetic and copies ran while one was open for 1% of the time, Pallas kernels for 0%

commit v1 on v0

v1 whole, which is shorter than its diff:
```python
import functools
import math

import jax
import jax.numpy as jnp
from jax import lax
from jax.experimental import pallas as pl
from jax.experimental.pallas import tpu as pltpu
from jax.sharding import PartitionSpec as P

KN = 8
TILE = 128
WIN = 512
GX = 64
ZS = 4
SPAN = WIN + 128
CAP = 256
EXTRA = 16
F32 = jnp.float32
BF16 = jnp.bfloat16


def dot(a, b):
    return jnp.dot(a, b, preferred_element_type=F32)


def dot_nt(a, b):
    return lax.dot_general(a, b, (((1,), (1,)), ((), ())), preferred_element_type=F32)


def window_base(offset, cells):
    return jnp.minimum(offset // 128 * 128, cells - SPAN)


def gelu_parts(x):
    z = jnp.abs(x) * (2.0**-0.5)
    t = 1.0 / (1.0 + 0.3275911 * z)
    e = jnp.exp(-0.5 * x * x)
    poly = ((((1.061405429 * t - 1.453152027) * t + 1.421413741) * t - 0.284496736) * t + 0.254829592) * t
    tail = 0.5 * poly * e
    cdf = jnp.where(x < 0, tail, 1.0 - tail)
    return x * cdf, cdf + x * e * ((2.0 * math.pi) ** -0.5)


def prepare(tiles, cells, meta_ref, ids_ref, rel_ref, pos_ref, relp_ref):
    slab = meta_ref[tiles]
    lives = []
    for t in range(tiles):
        cols = slice(t * TILE, (t + 1) * TILE)
        lives.append(jnp.where(ids_ref[:, cols] == slab, 1.0, 0.0))
        shift = meta_ref[t] - window_base(meta_ref[t], cells) + 1
        relp_ref[t * KN : (t + 1) * KN, :] = (rel_ref[:, cols] + shift).astype(F32)
    live = jnp.concatenate(lives, 0)
    rows = tiles * KN
    packed = live.astype(BF16)
    tri = jnp.where(
        lax.broadcasted_iota(jnp.int32, (TILE, TILE), 0) < lax.broadcasted_iota(jnp.int32, (TILE, TILE), 1), 1.0, 0.0
    ).astype(BF16)
    before = dot(packed, tri)
    total = dot(packed, jnp.ones((TILE, TILE), BF16))
    r = lax.broadcasted_iota(jnp.int32, (rows, rows), 0)
    c = lax.broadcasted_iota(jnp.int32, (rows, rows), 1)
    low = jnp.where((r // KN == c // KN) & (c < r), 1.0, 0.0).astype(BF16)
    start = dot(low, total.astype(BF16))
    pos_ref[...] = jnp.where(live > 0, before + start, -1.0e6)
    most = jnp.max(start + total).astype(jnp.int32)
    return (most + CAP - 1) // CAP


def pack_tile(t, c, base, slab, data_ref, pos_ref, relp_ref):
    channels = data_ref.shape[0] - EXTRA
    rows = pl.ds(pl.multiple_of(t * KN, KN), KN)
    pos = pos_ref[rows, :] - (c * CAP).astype(F32)
    relp = relp_ref[rows, :]
    place = lax.broadcasted_iota(jnp.int32, (CAP, TILE), 0).astype(F32)
    found = jnp.zeros((CAP, TILE), F32)
    for k in range(KN):
        found = jnp.where(pos[k : k + 1, :] == place, relp[k : k + 1, :], found)
    high = found.astype(BF16)
    low = (found - high.astype(F32)).astype(BF16)
    pick = jnp.where(found > 0, 1.0, 0.0).astype(BF16)
    drawn = dot_nt(data_ref[:, pl.ds(pl.multiple_of(t * TILE, TILE), TILE)], pick)
    ones = jnp.ones((8, TILE), BF16)
    spot = (dot_nt(ones, high) + dot_nt(ones, low)).astype(jnp.int32) - 1
    cell = spot + base
    along = [cell // (GX * ZS), cell // ZS % GX, cell % ZS + slab * ZS]
    along = [(a.astype(F32) + 0.5) / GX for a in along]
    row = lax.broadcasted_iota(jnp.int32, (8, CAP), 0)
    centre = jnp.where(row < 6, jnp.where(row % 3 == 0, along[0], jnp.where(row % 3 == 1, along[1], along[2])), 0.0)
    centre = jnp.concatenate([centre, jnp.zeros((8, CAP), F32)], 0)
    inputs = jnp.concatenate([drawn[channels:], centre], 0).astype(BF16)
    onehot = jnp.where(lax.broadcasted_iota(jnp.int32, (SPAN, CAP), 0) == spot[:1, :], 1.0, 0.0).astype(BF16)
    return drawn[:channels], inputs, onehot


def forward_kernel(tiles, group, meta_ref, data_ref, ids_ref, rel_ref, w1_ref, w2_ref, out_ref, pos_ref, relp_ref, grid_ref):
    cells = grid_ref.shape[1]
    chunks = prepare(tiles, cells, meta_ref, ids_ref, rel_ref, pos_ref, relp_ref)
    slab = meta_ref[tiles]

    grid_ref[...] = jnp.zeros_like(grid_ref)

    def body(i, _):
        c, g = i // (tiles // group), i % (tiles // group)
        done = []
        for u in range(group):
            t = g * group + u
            base = window_base(meta_ref[t], cells)
            cot, inputs, onehot = pack_tile(t, c, base, slab, data_ref, pos_ref, relp_ref)
            hidden = gelu_parts(dot(w1_ref[...], inputs))[0].astype(BF16)
            kernel = dot(w2_ref[...], jnp.concatenate([hidden, inputs], 0))
            done.append((base, dot_nt((kernel * cot).astype(BF16), onehot)))
        for base, part in done:
            at = pl.ds(pl.multiple_of(base, 128), SPAN)
            grid_ref[:, at] += part
        return 0

    lax.fori_loop(0, chunks * (tiles // group), body, 0)
    owned = out_ref.shape[2]
    for p in range(out_ref.shape[0]):
        out_ref[p] = grid_ref[:, p * owned : (p + 1) * owned].astype(out_ref.dtype)


def backward_kernel(tiles, group, meta_ref, data_ref, ids_ref, rel_ref, w1_ref, w2t_ref, feats_ref, out_ref, pos_ref, relp_ref):
    cells = feats_ref.shape[1]
    chunks = prepare(tiles, cells, meta_ref, ids_ref, rel_ref, pos_ref, relp_ref)
    slab = meta_ref[tiles]

    out_ref[...] = jnp.zeros_like(out_ref)

    def body(i, _):
        c, g = i // (tiles // group), i % (tiles // group)
        sums = []
        for u in range(group):
            t = g * group + u
            base = window_base(meta_ref[t], cells)
            cot, inputs, onehot = pack_tile(t, c, base, slab, data_ref, pos_ref, relp_ref)
            hidden, slope = gelu_parts(dot(w1_ref[...], inputs))
            feats = dot(feats_ref[:, pl.ds(pl.multiple_of(base, 128), SPAN)], onehot)
            grad_kernel = (feats * cot).astype(BF16)
            grad_pre = (dot(w2t_ref[...], grad_kernel) * slope).astype(BF16)
            sums.append(
                dot_nt(
                    jnp.concatenate([grad_kernel, grad_pre], 0),
                    jnp.concatenate([hidden.astype(BF16), inputs], 0),
                )
            )
        out_ref[...] += functools.reduce(lambda a, b: a + b, sums)
        return 0

    lax.fori_loop(0, chunks * (tiles // group), body, 0)


def split(values, parts):
    pieces = []
    for _ in range(parts):
        piece = lax.reduce_precision(values, 8, 7)
        pieces.append(piece.astype(BF16))
        values = values - piece
    return pieces


def shards(query_points, cotangent, slab_ids, rel_cells, offsets, latent, w_in, b_in, w_out, b_out):
    n_pb = lax.axis_size("pb")
    channels, owned = latent.shape[1], latent.shape[2]
    hid = w_in.shape[0]
    queries_dev = query_points.shape[1]
    tiles = queries_dev // TILE
    group = math.gcd(tiles, 4)
    cells = owned * n_pb

    slab_feats = lax.all_gather(latent[0], "pb", axis=1, tiled=True)

    meta = jnp.concatenate([offsets[0], lax.axis_index("ga")[None].astype(jnp.int32)])
    p_hi, p_lo = split(query_points, 2)
    ones = jnp.ones((3, queries_dev), BF16)
    data = jnp.concatenate([cotangent, p_hi, p_lo, p_hi, ones, jnp.zeros((EXTRA - 12, queries_dev), BF16)], 0)
    w_hi, w_lo = split(w_in, 2)
    b_parts = jnp.stack(split(b_in, 3), 1)
    w1 = jnp.concatenate(
        [w_hi[:, :3], w_hi[:, :3], w_lo[:, :3], b_parts, jnp.zeros((hid, EXTRA - 12), BF16),
         w_hi[:, 3:], w_lo[:, 3:], jnp.zeros((hid, 10), BF16)], 1)
    bo_parts = jnp.stack(split(b_out, 3), 1)
    w2 = jnp.concatenate(
        [w_out, jnp.zeros((channels, 9), BF16), bo_parts, jnp.zeros((channels, EXTRA + 4), BF16)], 1)

    vmem = pl.BlockSpec(memory_space=pltpu.VMEM)
    smem = pl.BlockSpec(memory_space=pltpu.SMEM)
    scratch = [pltpu.VMEM((tiles * KN, TILE), F32), pltpu.VMEM((tiles * KN, TILE), F32)]
    partial_grad = pl.pallas_call(
        functools.partial(forward_kernel, tiles, group),
        out_shape=jax.ShapeDtypeStruct((n_pb, channels, owned), BF16),
        in_specs=[smem] + [vmem] * 5,
        out_specs=vmem,
        scratch_shapes=scratch + [pltpu.VMEM((channels, cells), F32)],
        cost_estimate=pl.CostEstimate(flops=10**10, bytes_accessed=10**7, transcendentals=0),
        compiler_params=pltpu.CompilerParams(vmem_limit_bytes=40 * 2**20),
        name="forward",
    )(meta, data, slab_ids, rel_cells, w1, w2)
    received = lax.psum_scatter(partial_grad, "pb", scatter_dimension=0, tiled=True)
    sums = pl.pallas_call(
        functools.partial(backward_kernel, tiles, group),
        out_shape=jax.ShapeDtypeStruct((channels + hid, hid + EXTRA + 16), F32),
        in_specs=[smem] + [vmem] * 6,
        out_specs=vmem,
        scratch_shapes=scratch,
        cost_estimate=pl.CostEstimate(flops=10**10, bytes_accessed=10**7, transcendentals=0),
        compiler_params=pltpu.CompilerParams(vmem_limit_bytes=40 * 2**20),
        name="backward",
    )(meta, data, slab_ids, rel_cells, w1, w_out.T, slab_feats)
    scale = float(queries_dev * n_pb) ** (-0.5)
    sums = lax.psum(sums, ("pb", "ga")) * scale
    low = sums[channels:, hid:]
    w_in_grad = jnp.concatenate([low[:, 0:3] + low[:, 3:6], low[:, EXTRA : EXTRA + 3]], 1)
    return (
        received.astype(F32),
        w_in_grad,
        low[:, 9],
        sums[:channels, :hid],
        sums[:channels, hid + 9],
    )


def solution(mesh):
    return jax.shard_map(
        shards,
        mesh=mesh,
        in_specs=(
            P(None, "pb"),
            P(None, "pb"),
            P(None, "pb"),
            P(None, "pb"),
            P("ga", "pb"),
            P("ga", None, "pb"),
            P(),
            P(),
            P(),
            P(),
        ),
        out_specs=(P("ga", None, "pb"), P(), P(), P(), P()),
        check_vma=False,
    )
```

time: 465 us -> 184 us (0.40)
  local copies, waits for them, and re-layouts: 149 us -> 9.44 us
  matrix products: 112 us -> 0 us
  loops' own time: 62.8 us -> 0 us
  Pallas kernels: 0 us -> 42 us
  other arithmetic: 44.2 us -> 6.13 us
  waiting for transfers between devices: 38.4 us -> 71.8 us
    dot_general x48 -> x0, matrix products: 112 us -> none  [the longest x8 43 us: tile_work(): jnp.dot(w_in, features_in, precision=lax.Precision.HIGHEST, preferred_ele...]
    gather x96 -> x0, local copies, waits for them, and re-layouts: 70.8 us -> none
    another operation x9 -> x0, loops' own time: 62.8 us -> none  [the longest x1 62.1 us: shards(): lax.scan(advance, (start_grid, start_totals), inputs_all)]
    dynamic_update_slice x32 -> x0, local copies, waits for them, and re-layouts: 59.2 us -> none  [advance(): lax.dynamic_update_slice_in_dim(partial_grad, current + results[0][number...]
    pallas_call x0 -> x2, Pallas kernels: none -> 42 us  [the longest x1 22.6 us: shards(): pl.pallas_call(functools.partial(forward_kernel, tiles, group), out_shape...]
    reduce_scatter x1, waiting for transfers between devices: 9.53 us -> 43.1 us  [shards(): lax.psum_scatter(partial_grad, 'pb', scatter_dimension=0, tiled=True)]
    add x48 -> x1, other arithmetic: 33.1 us -> 0.09 us  [shards(): low[:, 0:3] + low[:, 3:6]]
    dynamic_slice x16 -> x0, local copies, waits for them, and re-layouts: 6.02 us -> none  [shards(): lax.scan(advance, (start_grid, start_totals), inputs_all)]
where the time goes in v1:
time: 184 us
  waiting for transfers between devices  71.8 us (39%)
  Pallas kernels  42 us (23%)
  blocking collectives  40 us (22%)
  between operations  14.2 us (8%)
  local copies, waits for them, and re-layouts  9.44 us (5%)
  other arithmetic  6.13 us (3%)
    reduce_scatter x1, waiting for transfers between devices, shards(): lax.psum_scatter(partial_grad, 'pb', scatter_dimension=0, tiled=True)  43.1 us
    psum x1, blocking collectives, shards(): sums = lax.psum(sums, ('pb', 'ga')) * scale  40 us
    all_gather x1, waiting for transfers between devices, shards(): slab_feats = lax.all_gather(latent[0], 'pb', axis=1, tiled=True)  27.9 us
    pallas_call x1, Pallas kernels, shards(): pl.pallas_call(functools.partial(forward_kernel, tiles, group), out_shape...  22.6 us
    pallas_call x1, Pallas kernels, shards(): pl.pallas_call(functools.partial(backward_kernel, tiles, group), out_shap...  19.4 us
  transfers between devices with their start and end apart: 2, of which 2 were waited for; matrix products, arithmetic and copies ran while one was open for 1% of the time, Pallas kernels for 0%

profile of v1, /device:TPU:0, one launch (start us, length us, event | category | flops | bytes accessed | tf_op | source)
XLA Modules:
  0.0 183.5 jit_solution(10147778914968088969)
XLA Ops:
  7.2 0.0 reduce-scatter.2.cloned.1.call-start
  7.2 0.7 fusion.3
  7.9 0.7 fusion.8
  8.6 0.3 concatenate.17
  8.9 0.1 copy.38.w1_ref
  9.0 0.9 fusion.1
  9.9 0.7 fusion.13
  10.5 0.1 copy.35
  10.6 0.1 copy.36
  10.7 0.1 copy.37
  10.9 0.7 pad_add_fusion.meta_ref
  11.6 2.2 %concatenate.16.data_ref = bf16[80,4096]{1,0:T(8,128)(2,1)S(1)} concatenate(bf16[64,4096]{1,0:T(8,128)(2,1)} %param.11, bf16[3,4096]{1,0:T(4,128)(2,1)S(1)} %get-tuple-element.18, bf16[3,4096]{1,0:T(4,128)(2,1)S(1)} %get-tuple-element.17, bf16[3,4096]{1,0:T(4,128)(2,1)S(1)} %get-tuple-element.18, bf16[3,4096]{1,0:T(4,128)(2,1)S(1)} %broadcast_in_dim.22, ...), dimensions={0} | concatenate | bytes 1310720 | tf_op jit(solution)/shard_map/concatenate | solution.py:177
  13.9 0.8 concatenate.18.w2_ref
  14.7 0.9 copy-done.1
  15.6 0.9 copy-done.3
  16.5 22.6 %forward.1 = bf16[8,64,2048]{2,1,0:T(8,128)(2,1)} custom-call(s32[33]{0:T(128)S(1)} %pad_add_fusion.meta_ref, bf16[80,4096]{1,0:T(8,128)(2,1)S(1)} %concatenate.16.data_ref, s32[8,4096]{1,0:T(8,128)S(1)} %copy-done.1, s32[8,4096]{1,0:T(8,128)S(1)} %copy-done.3, bf16[80,32]{1,0:T(8,128)(2,1)S(1)} %copy.38.w1_ref, bf16[64,112]{1,0:T(8,128)(2,1)S(1)} %concatenate.18.w2_ref), custom_call_target="tpu_custom_call" | custom-call | flops 10000000000 | bytes 10000000 | tf_op jit(solution)/shard_map/forward/pallas_call | solution.py:190
  39.1 0.0 all-gather.3.cloned.1.call-start
  39.2 0.7 all-gather.3.cloned.1.call-update
  39.9 0.1 copy.39
  40.0 43.1 %reduce-scatter.2.cloned.1.call-done = bf16[1,64,2048]{2,1,0:T(8,128)(2,1)} async-done(((bf16[8,64,2048]{2,1,0:T(8,128)(2,1)}), bf16[1,64,2048]{2,1,0:T(8,128)(2,1)}) %reduce-scatter.2.cloned.1.call-update) | async-done | bytes 262160 | tf_op jit(solution)/shard_map/reduce_scatter | solution.py:200
  83.1 1.8 convert_element_type.43
  84.9 27.9 %all-gather.3.cloned.1.call-done = bf16[1,64,16384]{2,1,0:T(8,128)(2,1)} async-done(((bf16[1,64,2048]{2,1,0:T(8,128)(2,1)}), bf16[1,64,16384]{2,1,0:T(8,128)(2,1)}) %all-gather.3.cloned.1.call-update) | async-done | bytes 2097168 | tf_op jit(solution)/shard_map/all_gather | solution.py:172
  112.8 1.6 copy-done
  114.4 19.4 %backward.1 = f32[144,112]{1,0:T(8,128)S(1)} custom-call(s32[33]{0:T(128)S(1)} %pad_add_fusion.meta_ref, bf16[80,4096]{1,0:T(8,128)(2,1)S(1)} %concatenate.16.data_ref, s32[8,4096]{1,0:T(8,128)S(1)} %copy-done.2, s32[8,4096]{1,0:T(8,128)S(1)} %copy-done.4, bf16[80,32]{1,0:T(8,128)(2,1)S(1)} %copy.38.w1_ref, bf16[80,64]{1,0:T(8,128)(2,1)S(1)} %bitcast.16, ...), custom_call_target="tpu_custom_call" | custom-call | flops 10000000000 | bytes 10000000 | tf_op jit(solution)/shard_map/backward/pallas_call | solution.py:201
  133.8 40.0 %psum.7 = f32[144,112]{1,0:T(8,128)S(1)} all-reduce(f32[144,112]{1,0:T(8,128)S(1)} %backward.1), channel_id=1, replica_groups=mesh['pb'=8,'ga'=4] {'pb','ga'}, use_global_device_ids=true, to_apply=%region_1.0 | all-reduce | flops 16128 | bytes 129024 | tf_op jit(solution)/shard_map/psum | solution.py:212
  173.8 0.1 slice_add_fusion
  173.9 0.6 slice.50
  174.5 0.7 slice_reduce_fusion
  175.2 0.7 slice_reduce_fusion.1
  175.9 0.1 copy.41
  176.0 0.1 copy.42
  176.1 0.6 pad_maximum_fusion
  (18 shorter events, 0.1 us)
Async XLA Ops:
  7.2 76.0 %reduce-scatter.2.cloned.1.call-start = ((), (), s32[]{:S(2)}) async-start(), calls=%async_computation.1 | async-start | bytes 2359296 | tf_op jit(solution)/shard_map/reduce_scatter | solution.py:200
  14.7 0.9 copy-start.1
  15.6 0.9 copy-start.3
  39.1 0.8 copy-start.5
  39.1 73.7 %copy-start.2 = (s32[8,4096]{1,0:T(8,128)S(1)}, s32[8,4096]{1,0:T(8,128)}, u32[]{:S(2)}) copy-start(s32[8,4096]{1,0:T(8,128)} %ids_ref.3) | copy-start | bytes 393220
  39.1 73.7 %copy-start.4 = (s32[8,4096]{1,0:T(8,128)S(1)}, s32[8,4096]{1,0:T(8,128)}, u32[]{:S(2)}) copy-start(s32[8,4096]{1,0:T(8,128)} %rel_ref.3) | copy-start | bytes 393220
  39.1 73.7 %all-gather.3.cloned.1.call-start = ((), (), s32[]{:S(2)}) async-start(), calls=%async_computation.2 | async-start | bytes 2359296 | tf_op jit(solution)/shard_map/all_gather | solution.py:172
  112.8 1.6 copy-start
Sparse Core Ops, SparseCore 0:
  39.3 43.8 reduce-scatter.1
  85.0 27.7 all-gather.2
